TPU v7x, 128 devices: a whole 4x4x4 slice. The times are simulated.
128 devices in a mesh: tok: 16 (over x, y_lo, core), col: 8 (over y_hi, z).
Axes of the slice: x: 4, y: 4 (y_hi: 2, y_lo: 2; y = y_hi * 2 + y_lo), z: 4, core: 2. Of those that a mesh axis runs over, the one named last changes fastest.
Arguments:
- activations: bfloat16 [2, 24576, 4096], P(None, 'tok', 'col'), may hold values from -6 to 6
- out_grads: bfloat16 [2, 24576, 4096], P(None, 'tok', 'col'), may hold values from -0.059814453 to 0.059814453
- token_mask: int32 [2, 24576], P(None, 'tok'), may hold values 0 or 1
- row_signs: int32 [4096], P('tok'), may hold values from 0 to 1
- col_signs: int32 [4096], P('col'), may hold values from 0 to 1
- bank: float32 [16, 4096, 4096], P(None, 'tok', 'col'), may hold values from -6 to 6
- bank_index: int32 [2], replicated, may hold values from 0 to 15, as said below
Outputs:
- fingerprints: float32 [2, 4096, 4096], P(None, 'tok', 'col')
- scores: float32 [2], replicated
Inputs may be any that keep to these rules, and one draw needn't show every extreme that they name: `bank_index`: the 2 values are distinct, and one of them is 15.
All inputs are finite; a program needn't handle non-finite values. No bound on the sum of `token_mask` on one device may be relied on, other than what follows from the above.
Results may differ from a plain program's by a relative error of at most 0.0003.
Values may be sent and summed in bfloat16 or wider, within the bound.
A program may use at most 128 MiB of HBM per device.

v0:
```python
import functools
import math
import jax
import jax.numpy as jnp
from jax import lax
from jax.sharding import Mesh
from jax.sharding import PartitionSpec as P

D = 4096
TOK = ("tok_0", "tok_1", "tok_2")
COL = ("col_0", "col_1")
TOK_COL = ("tok_0", "tok_1", "tok_2", "col_0", "col_1")
HIGH = lax.Precision.HIGHEST


def copy_for_each(x, axis):
    peers = lax.axis_size(axis)
    return lax.all_to_all(jnp.broadcast_to(x[None], (peers, *x.shape)), axis, 0, 0, tiled=True)


def joined_along(pieces, dim):
    lengths = list(pieces.shape[1:])
    lengths[dim] *= pieces.shape[0]
    return jnp.moveaxis(pieces, 0, dim).reshape(lengths)


def gathered_copies(x, axis, dim):
    pieces = copy_for_each(x, axis)
    return joined_along(pieces, dim)


def one_axis_at_a_time(x, axes):
    return functools.reduce(lax.psum, axes, x)


def hadamard(order):
    positions = jnp.arange(order, dtype=jnp.int32)
    common_bits = jnp.bitwise_and(positions[:, None], positions[None, :])
    parity = jnp.zeros((order, order), jnp.int32)
    for bit_number in range(max(order.bit_length() - 1, 0)):
        parity = parity + jnp.bitwise_and(jnp.right_shift(common_bits, bit_number), 1)
    return (1 - 2 * (parity % 2)).astype(jnp.float32)


def body(activations, out_grads, token_mask, row_signs, col_signs, bank, bank_index):
    row_pm = (2 * row_signs - 1).astype(jnp.float32)
    col_pm = (2 * col_signs - 1).astype(jnp.float32)
    tok_count = lax.axis_size(TOK)
    col_count = lax.axis_size(COL)
    local_rows = row_pm.shape[0]
    local_cols = col_pm.shape[0]
    tok_table = hadamard(tok_count)
    col_table = hadamard(col_count)
    rows_table = hadamard(local_rows)
    cols_table = hadamard(local_cols)
    factor = 1.0 / math.sqrt(D)
    squared = float(D) * float(D)
    all_signs = gathered_copies(row_signs, TOK, 0)
    full_pm = (2 * all_signs - 1).astype(jnp.float32)
    prints = []
    crosses = []
    owns = []
    refsqs = []
    for seq_number in range(activations.shape[0]):
        features = lax.all_gather(activations[seq_number], COL, axis=1, tiled=True)
        masked = out_grads[seq_number] * token_mask[seq_number][:, None].astype(jnp.bfloat16)
        partial_value = jnp.einsum(
            "tr,tc->rc", features, masked, preferred_element_type=jnp.float32
        )
        blocks = (partial_value * full_pm[:, None]).reshape(tok_count, local_rows, local_cols)
        blocks = jnp.einsum("rs,asc->arc", rows_table, blocks, precision=HIGH)
        blocks = jnp.einsum("ab,brc->arc", tok_table, blocks, precision=HIGH)
        premixed = blocks.reshape(tok_count * local_rows, local_cols)

        def term_rows(row_start, row_count, premixed=premixed):
            return premixed

        summed = lax.psum_scatter(
            term_rows(jnp.int32(0), lax.axis_size(TOK) * local_rows),
            TOK,
            scatter_dimension=0,
            tiled=True,
        )
        slab = summed
        slab = slab * factor
        slab = jnp.dot(slab * col_pm[None, :], cols_table, precision=HIGH)
        pieces = slab.reshape(col_count, local_rows // col_count, local_cols)
        col_pieces = lax.all_to_all(pieces, COL, split_axis=0, concat_axis=0, tiled=True)
        mixed_cols = jnp.einsum("ab,brc->arc", col_table, col_pieces, precision=HIGH)
        pieces = lax.all_to_all(mixed_cols, COL, split_axis=0, concat_axis=0, tiled=True)
        slab = pieces.reshape(local_rows, local_cols)
        slab = slab * factor
        chosen = lax.dynamic_index_in_dim(bank, bank_index[seq_number], 0, keepdims=False)
        prints.append(slab)
        crosses.append(jnp.sum(slab * chosen))
        owns.append(jnp.sum(slab * slab))
        refsqs.append(jnp.sum(chosen * chosen))
    cross, own, refsq = (
        one_axis_at_a_time(jnp.stack(crosses), TOK_COL),
        one_axis_at_a_time(jnp.stack(owns), TOK_COL),
        one_axis_at_a_time(jnp.stack(refsqs), TOK_COL),
    )
    scores = D * (cross / squared) / jnp.sqrt((own / squared + 1e-06) * (refsq / squared + 1e-06))
    return (jnp.stack(prints), scores)


def solution(mesh):
    split = Mesh(mesh.devices.reshape(4, 2, 2, 2, 4), ("tok_0", "tok_1", "tok_2", "col_0", "col_1"))
    return jax.shard_map(
        body,
        mesh=split,
        in_specs=(
            P(None, TOK, COL),
            P(None, TOK, COL),
            P(None, TOK),
            P(TOK),
            P(COL),
            P(None, TOK, COL),
            P(),
        ),
        out_specs=(P(None, TOK, COL), P()),
        check_vma=False,
    )
```

profile of v0, /device:TPU:0, one launch (start us, length us, event | category | flops | bytes accessed | tf_op | source)
XLA Modules:
  0.0 617.7 jit_solution(9460281022073052252)
XLA Ops:
  7.2 4.0 fusion.135
  11.3 0.7 all-gather.5.cloned.1.call-update
  12.0 0.6 broadcast_in_dim.2
  12.6 5.5 all-to-all-start
  18.3 6.0 all-to-all-done
  24.3 142.2 %all-gather.7.cloned.1.call-done = bf16[1,1536,4096]{2,1,0:T(8,128)(2,1)} async-done(((bf16[1,1536,512]{2,1,0:T(8,128)(2,1)}), bf16[1,1536,4096]{2,1,0:T(8,128)(2,1)}) %all-gather.7.cloned.1.call-update) | async-done | bytes 12582928 | tf_op jit(solution)/shard_map/all_gather | solution.py:65
  166.5 10.4 %fusion.7 = f32[512,4096]{1,0:T(8,128)S(1)} fusion(bf16[1,1536,4096]{2,1,0:T(8,128)(2,1)} %all-gather.7.cloned.1.call-done, f32[4096]{0:T(1024)S(1)} %bitcast.87, bf16[2,1536,512]{2,1,0:T(8,128)(2,1)S(1)} %copy-done.4, bf16[1536]{0:T(1024)(128)(2,1)S(1)} %get-tuple-element.7), kind=kOutput, calls=%fused_computation.5 | convolution fusion | flops 6445334528 | bytes 22564864 | tf_op jit(solution)/shard_map/tr,tc->rc/dot_general | solution.py:67
  176.9 3.9 copy.28
  180.8 9.6 %convolution_bitcast_fusion = f32[16,256,512]{1,0,2:T(8,128)} fusion(f32[16,256,512]{1,0,2:T(8,128)S(1)} %bitcast.81), kind=kOutput, calls=%fused_computation.6 | convolution fusion | flops 6444941312 | bytes 16777216 | tf_op jit(solution)/shard_map/rs,asc->arc/dot_general | solution.py:71
  190.4 10.5 %copy.23 = f32[16,256,512]{2,0,1:T(8,128)} copy(f32[16,256,512]{1,0,2:T(8,128)} %convolution_bitcast_fusion) | data formatting | bytes 16777216 | tf_op jit(solution)/shard_map/rs,asc->arc/transpose | solution.py:71
  200.9 11.6 %fusion.62 = f32[16,256,512]{2,0,1:T(8,128)S(1)} fusion(f32[16,256,512]{2,0,1:T(8,128)} %copy.23), kind=kOutput, calls=%fused_computation.77 | convolution fusion | flops 402659840 | bytes 16777216 | tf_op jit(solution)/shard_map/ab,brc->arc/dot_general | solution.py:72
  212.5 8.0 %copy.24 = f32[16,256,512]{2,1,0:T(8,128)} copy(f32[16,256,512]{2,0,1:T(8,128)S(1)} %fusion.62) | data formatting | bytes 16777216 | tf_op jit(solution)/shard_map/ab,brc->arc/dot_general | solution.py:72
  220.6 98.5 %all-gather.5.cloned.1.call-done = bf16[1,1536,4096]{2,1,0:T(8,128)(2,1)} async-done(((bf16[1,1536,512]{2,1,0:T(8,128)(2,1)}), bf16[1,1536,4096]{2,1,0:T(8,128)(2,1)}) %all-gather.5.cloned.1.call-update) | async-done | bytes 12582928 | tf_op jit(solution)/shard_map/all_gather | solution.py:65
  319.1 10.6 %fusion.4 = f32[512,4096]{1,0:T(8,128)S(1)} fusion(bf16[1,1536,4096]{2,1,0:T(8,128)(2,1)} %all-gather.5.cloned.1.call-done, f32[4096]{0:T(1024)S(1)} %bitcast.88, bf16[2,1536,512]{2,1,0:T(8,128)(2,1)S(1)} %copy-done.4, bf16[1536]{0:T(1024)(128)(2,1)S(1)} %get-tuple-element.6), kind=kOutput, calls=%fused_computation.4 | convolution fusion | flops 6445334528 | bytes 22564864 | tf_op jit(solution)/shard_map/tr,tc->rc/dot_general | solution.py:67
  329.6 3.9 copy.27
  333.5 9.6 %convolution_bitcast_fusion.1 = f32[16,256,512]{1,0,2:T(8,128)} fusion(f32[16,256,512]{1,0,2:T(8,128)S(1)} %bitcast.82), kind=kOutput, calls=%fused_computation.7 | convolution fusion | flops 6444941312 | bytes 16777216 | tf_op jit(solution)/shard_map/rs,asc->arc/dot_general | solution.py:71
  343.2 10.5 %copy.19 = f32[16,256,512]{2,0,1:T(8,128)} copy(f32[16,256,512]{1,0,2:T(8,128)} %convolution_bitcast_fusion.1) | data formatting | bytes 16777216 | tf_op jit(solution)/shard_map/rs,asc->arc/transpose | solution.py:71
  353.7 11.8 %fusion.64 = f32[16,256,512]{2,0,1:T(8,128)S(1)} fusion(f32[16,256,512]{2,0,1:T(8,128)} %copy.19), kind=kOutput, calls=%fused_computation.78 | convolution fusion | flops 402659840 | bytes 16777216 | tf_op jit(solution)/shard_map/ab,brc->arc/dot_general | solution.py:72
  365.5 8.1 %copy.20 = f32[16,256,512]{2,1,0:T(8,128)} copy(f32[16,256,512]{2,0,1:T(8,128)S(1)} %fusion.64) | data formatting | bytes 16777216 | tf_op jit(solution)/shard_map/ab,brc->arc/dot_general | solution.py:72
  373.6 0.7 copy-done.1
  374.2 41.1 %reduce-scatter.5.cloned.1.call-done = f32[256,512]{1,0:T(8,128)} async-done(((f32[4096,512]{1,0:T(8,128)}), f32[256,512]{1,0:T(8,128)}) %reduce-scatter.5.cloned.1.call-update) | async-done | bytes 524304 | tf_op jit(solution)/shard_map/reduce_scatter | solution.py:78
  415.3 4.3 fusion.26
  419.7 4.9 all-to-all-start.3
  424.6 92.7 %reduce-scatter.3.cloned.1.call-done = f32[256,512]{1,0:T(8,128)} async-done(((f32[4096,512]{1,0:T(8,128)}), f32[256,512]{1,0:T(8,128)}) %reduce-scatter.3.cloned.1.call-update) | async-done | bytes 524304 | tf_op jit(solution)/shard_map/reduce_scatter | solution.py:78
  517.3 4.3 fusion.29
  521.6 7.2 %all-to-all-start.1 = ((f32[8,32,512]{2,1,0:T(8,128)}), f32[8,32,512]{2,1,0:T(8,128)S(1)}, u32[]{:S(2)}, u32[]{:S(2)}) async-start(f32[8,32,512]{2,1,0:T(8,128)} %bitcast.9), calls=%async_computation.2 | async-start | bytes 1048576 | tf_op jit(solution)/shard_map/all_to_all | solution.py:88
  528.8 0.8 fusion.22
  529.6 1.1 copy.26
  530.7 9.4 %all-to-all-done.1 = f32[8,32,512]{2,1,0:T(8,128)S(1)} async-done(((f32[8,32,512]{2,1,0:T(8,128)}), f32[8,32,512]{2,1,0:T(8,128)S(1)}, u32[]{:S(2)}, u32[]{:S(2)}) %all-to-all-start.1) | async-done | bytes 524320 | tf_op jit(solution)/shard_map/all_to_all | solution.py:88
  540.1 4.4 all-to-all-start.4
  544.5 0.8 fusion.24
  545.3 1.1 copy.22
  546.4 9.3 %all-to-all-done.4 = f32[8,32,512]{2,1,0:T(8,128)S(1)} async-done(((f32[8,32,512]{2,1,0:T(8,128)}), f32[8,32,512]{2,1,0:T(8,128)S(1)}, u32[]{:S(2)}, u32[]{:S(2)}) %all-to-all-start.4) | async-done | bytes 524320 | tf_op jit(solution)/shard_map/all_to_all | solution.py:90
  555.6 3.5 all-to-all-start.2
  559.2 0.6 fusion.136
  563.6 0.7 multiply_reduce_fusion
  564.4 5.8 all-to-all-done.2
  570.2 0.8 multiply_reduce_fusion.1
  571.0 1.0 pad_maximum_fusion
  572.0 2.0 fusion.20
  574.1 1.3 pad_maximum_fusion.3
  575.4 2.6 pad_maximum_fusion.1
  578.0 9.7 %all-reduce.1 = (f32[2]{0:T(128)S(1)}, f32[2]{0:T(128)S(1)}, f32[2]{0:T(128)S(1)}) all-reduce(f32[2]{0:T(128)S(1)} %pad_maximum_fusion.3, f32[2]{0:T(128)S(1)} %get-tuple-element.32, f32[2]{0:T(128)S(1)} %get-tuple-element.31), channel_id=1, replica_groups=mesh['tok_0'=4,'tok_1'=2,'tok_2'=2,'col_0'=2,'col_1'=4] {'tok_0'}, use_global_device_ids=true, to_apply=%region_18.19 | all-reduce | flops 6 | bytes 48 | tf_op jit(solution)/shard_map/psum | solution.py:33
  587.7 4.9 all-reduce.4
  592.6 2.4 all-reduce.3
  595.1 6.4 %all-reduce.2 = (f32[2]{0:T(128)S(1)}, f32[2]{0:T(128)S(1)}, f32[2]{0:T(128)S(1)}) all-reduce(f32[2]{0:T(128)S(1)} %get-tuple-element.17, f32[2]{0:T(128)S(1)} %get-tuple-element.18, f32[2]{0:T(128)S(1)} %get-tuple-element.19), channel_id=1, replica_groups=mesh['tok_0'=4,'tok_1'=2,'tok_2'=2,'col_0'=2,'col_1'=4] {'col_0'}, use_global_device_ids=true, to_apply=%region_21.22 | all-reduce | flops 6 | bytes 48 | tf_op jit(solution)/shard_map/psum | solution.py:33
  601.5 9.0 %all-reduce = (f32[2]{0:T(128)S(1)}, f32[2]{0:T(128)S(1)}, f32[2]{0:T(128)S(1)}) all-reduce(f32[2]{0:T(128)S(1)} %get-tuple-element.14, f32[2]{0:T(128)S(1)} %get-tuple-element.15, f32[2]{0:T(128)S(1)} %get-tuple-element.16), channel_id=1, replica_groups=mesh['tok_0'=4,'tok_1'=2,'tok_2'=2,'col_0'=2,'col_1'=4] {'col_1'}, use_global_device_ids=true, to_apply=%region_22.23 | all-reduce | flops 6 | bytes 48 | tf_op jit(solution)/shard_map/psum | solution.py:33
  610.5 0.5 rsqrt_multiply_fusion
  (21 shorter events, 0.3 us)
Async XLA Ops:
  7.2 4.8 copy-start.3
  7.2 11.0 %copy-start = (s32[2,1536]{1,0:T(2,128)S(1)}, s32[2,1536]{1,0:T(2,128)}, u32[]{:S(2)}) copy-start(s32[2,1536]{1,0:T(2,128)} %param.9) | copy-start | bytes 36868
  7.2 159.3 %copy-start.4 = (bf16[2,1536,512]{2,1,0:T(8,128)(2,1)S(1)}, bf16[2,1536,512]{2,1,0:T(8,128)(2,1)}, u32[]{:S(2)}) copy-start(bf16[2,1536,512]{2,1,0:T(8,128)(2,1)} %param.8) | copy-start | bytes 9437188
  7.2 159.3 %all-gather.7.cloned.1.call-start = ((), (), s32[]{:S(2)}) async-start(), calls=%async_computation.10 | async-start | bytes 14155776 | tf_op jit(solution)/shard_map/all_gather | solution.py:65
  11.2 307.8 %all-gather.5.cloned.1.call-start = ((), (), s32[]{:S(2)}) async-start(), calls=%async_computation.9 | async-start | bytes 14155776 | tf_op jit(solution)/shard_map/all_gather | solution.py:65
  12.6 11.6 %all-to-all-start = ((s32[16,1,256]{2,1,0:T(1,128)}), s32[16,1,256]{2,1,0:T(1,128)S(1)}, u32[]{:S(2)}, u32[]{:S(2)}) async-start(s32[16,1,256]{2,1,0:T(1,128)} %broadcast_in_dim.2), calls=%async_computation | async-start | bytes 32768 | tf_op jit(solution)/shard_map/all_to_all | solution.py:18
  18.1 397.2 %reduce-scatter.5.cloned.1.call-start = ((), (), s32[]{:S(2)}) async-start(), calls=%async_computation.8 | async-start | bytes 8912896 | tf_op jit(solution)/shard_map/reduce_scatter | solution.py:78
  220.5 296.8 %reduce-scatter.3.cloned.1.call-start = ((), (), s32[]{:S(2)}) async-start(), calls=%async_computation.7 | async-start | bytes 8912896 | tf_op jit(solution)/shard_map/reduce_scatter | solution.py:78
  373.5 0.7 copy-start.1
  419.7 102.0 %all-to-all-start.3 = ((f32[8,32,512]{2,1,0:T(8,128)}), f32[8,32,512]{2,1,0:T(8,128)S(1)}, u32[]{:S(2)}, u32[]{:S(2)}) async-start(f32[8,32,512]{2,1,0:T(8,128)} %bitcast.16), calls=%async_computation.5 | async-start | bytes 1048576 | tf_op jit(solution)/shard_map/all_to_all | solution.py:88
  424.6 134.6 %copy-start.2 = (s32[2]{0:T(128)S(1)}, s32[2]{0:T(128)}, u32[]{:S(2)}) copy-start(s32[2]{0:T(128)} %param.13) | copy-start | bytes 28
  521.6 18.5 %all-to-all-start.1 = ((f32[8,32,512]{2,1,0:T(8,128)}), f32[8,32,512]{2,1,0:T(8,128)S(1)}, u32[]{:S(2)}, u32[]{:S(2)}) async-start(f32[8,32,512]{2,1,0:T(8,128)} %bitcast.9), calls=%async_computation.2 | async-start | bytes 1048576 | tf_op jit(solution)/shard_map/all_to_all | solution.py:88
  540.1 15.5 %all-to-all-start.4 = ((f32[8,32,512]{2,1,0:T(8,128)}), f32[8,32,512]{2,1,0:T(8,128)S(1)}, u32[]{:S(2)}, u32[]{:S(2)}) async-start(f32[8,32,512]{2,1,0:T(8,128)} %copy.26), calls=%async_computation.6 | async-start | bytes 1048576 | tf_op jit(solution)/shard_map/all_to_all | solution.py:90
  555.6 14.5 %all-to-all-start.2 = ((f32[8,32,512]{2,1,0:T(8,128)}), f32[8,32,512]{2,1,0:T(8,128)S(1)}, u32[]{:S(2)}, u32[]{:S(2)}) async-start(f32[8,32,512]{2,1,0:T(8,128)} %copy.22), calls=%async_computation.3 | async-start | bytes 1048576 | tf_op jit(solution)/shard_map/all_to_all | solution.py:90
Sparse Core Ops, SparseCore 0:
  11.4 155.1 all-gather.6
  168.7 150.3 all-gather.4
  321.5 93.8 reduce-scatter.4
  417.6 99.6 reduce-scatter.2
where the time goes:
time: 628 us; the launch traced here: 618 us
  waiting for transfers between devices  406 us (65%)
  matrix products  73.7 us (12%)
  local copies, waits for them, and re-layouts  53 us (8%)
  blocking collectives  32.5 us (5%)
  starting transfers between devices  25.6 us (4%)
  between operations  18 us (3%)
  other arithmetic  9.12 us (1%)
    all_gather x2, waiting for transfers between devices, body(): features = lax.all_gather(activations[seq_number], COL, axis=1, tiled=True)  241 us
    reduce_scatter x2, waiting for transfers between devices, body(): lax.psum_scatter(term_rows(jnp.int32(0), lax.axis_size(TOK) * local_rows)...  134 us
    psum x5, blocking collectives, one_axis_at_a_time(): return functools.reduce(lax.psum, axes, x)  32.5 us
    dot_general x2, matrix products, body(): blocks = jnp.einsum('ab,brc->arc', tok_table, blocks, precision=HIGH)  23.4 us
    transpose x2, local copies, waits for them, and re-layouts, body(): blocks = jnp.einsum('rs,asc->arc', rows_table, blocks, precision=HIGH)  21 us
    dot_general x2, matrix products, body(): jnp.einsum('tr,tc->rc', features, masked, preferred_element_type=jnp.floa...  20.9 us
    dot_general x2, matrix products, body(): blocks = jnp.einsum('rs,asc->arc', rows_table, blocks, precision=HIGH)  19.2 us
    dot_general x2, local copies, waits for them, and re-layouts, body(): blocks = jnp.einsum('ab,brc->arc', tok_table, blocks, precision=HIGH)  16.1 us
  transfers between devices with their start and end apart: 9, of which 8 were waited for; matrix products, arithmetic and copies ran while one was open for 20% of the time, Pallas kernels for 0%

commit v1 on v0

--- a/solution.py
+++ b/solution.py
@@ -62,7 +62,10 @@
     owns = []
     refsqs = []
     for seq_number in range(activations.shape[0]):
-        features = lax.all_gather(activations[seq_number], COL, axis=1, tiled=True)
+        features = jnp.concatenate(
+            lax.all_to_all(jnp.stack([activations[seq_number]] * lax.axis_size(COL)), COL, 0, 0),
+            axis=1,
+        )
         masked = out_grads[seq_number] * token_mask[seq_number][:, None].astype(jnp.bfloat16)
         partial_value = jnp.einsum(
             "tr,tc->rc", features, masked, preferred_element_type=jnp.float32

time: 628 us -> 725 us (1.15)
  blocking collectives: 32.5 us -> 258 us
  waiting for transfers between devices: 406 us -> 253 us
  local copies, waits for them, and re-layouts: 53 us -> 70.3 us
    all_gather x2 -> x0, waiting for transfers between devices: 241 us -> none  [body(): features = lax.all_gather(activations[seq_number], COL, axis=1, tiled=True)]
    all_to_all x0 -> x1, blocking collectives: none -> 225 us  [body(): lax.all_to_all(jnp.stack([activations[seq_number]] * lax.axis_size(COL)),...]
    all_to_all x0 -> x1, waiting for transfers between devices: none -> 139 us  [body(): lax.all_to_all(jnp.stack([activations[seq_number]] * lax.axis_size(COL)),...]
    reduce_scatter x2, waiting for transfers between devices: 134 us -> 88.5 us  [body(): lax.psum_scatter(term_rows(jnp.int32(0), lax.axis_size(TOK) * local_rows)...]
    another operation x0 -> x2, local copies, waits for them, and re-layouts: none -> 11.1 us  [body(): jnp.stack([activations[seq_number]] * lax.axis_size(COL))]
    all_to_all x0 -> x1, starting transfers between devices: none -> 7.78 us  [body(): lax.all_to_all(jnp.stack([activations[seq_number]] * lax.axis_size(COL)),...]
  transfers between devices with their start and end apart: 9 -> 8, of which waited for: 8 -> 6; matrix products, arithmetic and copies ran while one was open for 20% -> 11% of each run, Pallas kernels for 0% -> 0%
where the time goes in v1:
time: 725 us; the launch traced here: 714 us
  blocking collectives  258 us (36%)
  waiting for transfers between devices  253 us (35%)
  matrix products  72.6 us (10%)
  local copies, waits for them, and re-layouts  70.3 us (10%)
  starting transfers between devices  32.6 us (4%)
  between operations  18.5 us (3%)
  other arithmetic  9.12 us (1%)
    all_to_all x1, blocking collectives, body(): lax.all_to_all(jnp.stack([activations[seq_number]] * lax.axis_size(COL)),...  225 us
    all_to_all x1, waiting for transfers between devices, body(): lax.all_to_all(jnp.stack([activations[seq_number]] * lax.axis_size(COL)),...  139 us
    reduce_scatter x2, waiting for transfers between devices, body(): lax.psum_scatter(term_rows(jnp.int32(0), lax.axis_size(TOK) * local_rows)...  88.5 us
    psum x5, blocking collectives, one_axis_at_a_time(): return functools.reduce(lax.psum, axes, x)  33 us
    dot_general x2, matrix products, body(): blocks = jnp.einsum('ab,brc->arc', tok_table, blocks, precision=HIGH)  22.9 us
    transpose x2, local copies, waits for them, and re-layouts, body(): blocks = jnp.einsum('rs,asc->arc', rows_table, blocks, precision=HIGH)  21.3 us
    dot_general x2, matrix products, body(): jnp.einsum('tr,tc->rc', features, masked, preferred_element_type=jnp.floa...  20.3 us
    dot_general x2, matrix products, body(): blocks = jnp.einsum('rs,asc->arc', rows_table, blocks, precision=HIGH)  19.2 us
  transfers between devices with their start and end apart: 8, of which 6 were waited for; matrix products, arithmetic and copies ran while one was open for 11% of the time, Pallas kernels for 0%

profile of v1, /device:TPU:0, one launch (start us, length us, event | category | flops | bytes accessed | tf_op | source)
XLA Modules:
  0.0 713.9 jit_solution(10503256583265065859)
XLA Ops:
  7.2 1.3 broadcast_in_dim.2
  8.5 5.5 all-to-all-start.1
  14.0 3.2 slice_bitcast_fusion.1
  17.2 1.7 copy.26
  19.0 1.1 all-to-all-done.1
  20.1 5.5 stack.39
  25.6 7.8 %all-to-all-start.4 = ((bf16[8,1536,512]{1,2,0:T(8,128)(2,1)}), bf16[8,1536,512]{1,2,0:T(8,128)(2,1)}, u32[]{:S(2)}, u32[]{:S(2)}) async-start(bf16[8,1536,512]{1,2,0:T(8,128)(2,1)} %stack.39), calls=%async_computation.5 | async-start | bytes 25165824 | tf_op jit(solution)/shard_map/all_to_all | solution.py:66
  33.6 139.0 %all-to-all-done.4 = bf16[8,1536,512]{1,2,0:T(8,128)(2,1)} async-done(((bf16[8,1536,512]{1,2,0:T(8,128)(2,1)}), bf16[8,1536,512]{1,2,0:T(8,128)(2,1)}, u32[]{:S(2)}, u32[]{:S(2)}) %all-to-all-start.4) | async-done | bytes 12582944 | tf_op jit(solution)/shard_map/all_to_all | solution.py:66
  172.6 10.8 %convolution_multiply_fusion = f32[512,4096]{1,0:T(8,128)S(1)} fusion(bf16[1536,4096]{0,1:T(8,128)(2,1)} %bitcast.16, f32[4096]{0:T(1024)S(1)} %bitcast.90, bf16[2,1536,512]{2,1,0:T(8,128)(2,1)} %param.8, bf16[1536]{0:T(1024)(128)(2,1)S(1)} %get-tuple-element.7), kind=kOutput, calls=%fused_computation | convolution fusion | flops 6445334528 | bytes 22563840 | tf_op jit(solution)/shard_map/tr,tc->rc/dot_general | solution.py:70
  183.4 3.9 copy.32
  187.3 9.6 %convolution_bitcast_fusion = f32[16,256,512]{1,0,2:T(8,128)} fusion(f32[16,256,512]{1,0,2:T(8,128)S(1)} %bitcast.83), kind=kOutput, calls=%fused_computation.2 | convolution fusion | flops 6444941312 | bytes 16777216 | tf_op jit(solution)/shard_map/rs,asc->arc/dot_general | solution.py:74
  196.9 10.8 %copy.27 = f32[16,256,512]{2,0,1:T(8,128)} copy(f32[16,256,512]{1,0,2:T(8,128)} %convolution_bitcast_fusion) | data formatting | bytes 16777216 | tf_op jit(solution)/shard_map/rs,asc->arc/transpose | solution.py:74
  207.7 11.4 %fusion.56 = f32[16,256,512]{2,0,1:T(8,128)S(1)} fusion(f32[16,256,512]{2,0,1:T(8,128)} %copy.27), kind=kOutput, calls=%fused_computation.77 | convolution fusion | flops 402659840 | bytes 16777216 | tf_op jit(solution)/shard_map/ab,brc->arc/dot_general | solution.py:75
  219.1 8.1 %copy.28 = f32[16,256,512]{2,1,0:T(8,128)} copy(f32[16,256,512]{2,0,1:T(8,128)S(1)} %fusion.56) | data formatting | bytes 16777216 | tf_op jit(solution)/shard_map/ab,brc->arc/dot_general | solution.py:75
  227.3 0.7 copy.21
  228.0 5.6 stack.38
  233.6 225.2 %all_to_all.36 = bf16[8,1536,512]{1,2,0:T(8,128)(2,1)S(1)} all-to-all(bf16[8,1536,512]{1,2,0:T(8,128)(2,1)} %stack.38), channel_id=1, replica_groups=mesh['tok_0'=4,'tok_1'=2,'tok_2'=2,'col_0'=2,'col_1'=4] {'col_0','col_1'}, dimensions={0} | all-to-all | bytes 25165824 | tf_op jit(solution)/shard_map/all_to_all | solution.py:66
  458.8 9.5 %convolution_multiply_fusion.1 = f32[512,4096]{1,0:T(8,128)} fusion(bf16[1536,4096]{0,1:T(8,128)(2,1)S(1)} %bitcast.85, f32[4096]{0:T(1024)S(1)} %bitcast.91, bf16[2,1536,512]{2,1,0:T(8,128)(2,1)S(1)} %copy-done.3, bf16[1536]{0:T(1024)(128)(2,1)S(1)} %get-tuple-element.6), kind=kOutput, calls=%fused_computation.1 | convolution fusion | flops 6445334528 | bytes 22564864 | tf_op jit(solution)/shard_map/tr,tc->rc/dot_general | solution.py:70
  468.3 7.3 %copy.31 = f32[64,8,16,256]{3,2,1,0:T(8,128)S(1)} copy(f32[64,8,16,256]{3,1,2,0:T(8,128)} %bitcast.86) | data formatting | bytes 16777216
  475.6 9.6 %convolution_bitcast_fusion.1 = f32[16,256,512]{1,0,2:T(8,128)} fusion(f32[16,256,512]{1,0,2:T(8,128)S(1)} %bitcast.84), kind=kOutput, calls=%fused_computation.3 | convolution fusion | flops 6444941312 | bytes 16777216 | tf_op jit(solution)/shard_map/rs,asc->arc/dot_general | solution.py:74
  485.1 10.5 %copy.22 = f32[16,256,512]{2,0,1:T(8,128)} copy(f32[16,256,512]{1,0,2:T(8,128)} %convolution_bitcast_fusion.1) | data formatting | bytes 16777216 | tf_op jit(solution)/shard_map/rs,asc->arc/transpose | solution.py:74
  495.6 11.6 %fusion.58 = f32[16,256,512]{2,0,1:T(8,128)S(1)} fusion(f32[16,256,512]{2,0,1:T(8,128)} %copy.22), kind=kOutput, calls=%fused_computation.78 | convolution fusion | flops 402659840 | bytes 16777216 | tf_op jit(solution)/shard_map/ab,brc->arc/dot_general | solution.py:75
  507.2 8.2 %copy.23 = f32[16,256,512]{2,1,0:T(8,128)} copy(f32[16,256,512]{2,0,1:T(8,128)S(1)} %fusion.58) | data formatting | bytes 16777216 | tf_op jit(solution)/shard_map/ab,brc->arc/dot_general | solution.py:75
  516.0 4.3 fusion.20
  520.4 3.7 all-to-all-start.5
  524.1 88.5 %reduce-scatter.3.cloned.1.call-done = f32[256,512]{1,0:T(8,128)} async-done(((f32[4096,512]{1,0:T(8,128)}), f32[256,512]{1,0:T(8,128)}) %reduce-scatter.3.cloned.1.call-update) | async-done | bytes 524304 | tf_op jit(solution)/shard_map/reduce_scatter | solution.py:81
  612.6 4.3 fusion.23
  616.9 7.0 all-to-all-start.2
  623.9 0.8 fusion.16
  624.7 1.1 copy.30
  625.8 8.7 %all-to-all-done.2 = f32[8,32,512]{2,1,0:T(8,128)S(1)} async-done(((f32[8,32,512]{2,1,0:T(8,128)}), f32[8,32,512]{2,1,0:T(8,128)S(1)}, u32[]{:S(2)}, u32[]{:S(2)}) %all-to-all-start.2) | async-done | bytes 524320 | tf_op jit(solution)/shard_map/all_to_all | solution.py:91
  634.6 5.0 all-to-all-start.6
  639.6 0.8 fusion.18
  640.4 1.1 copy.25
  641.5 9.3 %all-to-all-done.6 = f32[8,32,512]{2,1,0:T(8,128)S(1)} async-done(((f32[8,32,512]{2,1,0:T(8,128)}), f32[8,32,512]{2,1,0:T(8,128)S(1)}, u32[]{:S(2)}, u32[]{:S(2)}) %all-to-all-start.6) | async-done | bytes 524320 | tf_op jit(solution)/shard_map/all_to_all | solution.py:93
  650.8 3.5 all-to-all-start.3
  658.8 0.7 multiply_reduce_fusion
  659.5 5.7 all-to-all-done.3
  665.3 0.8 multiply_reduce_fusion.1
  666.1 1.0 pad_maximum_fusion
  667.1 2.0 fusion.14
  669.2 1.3 pad_maximum_fusion.3
  670.5 2.6 pad_maximum_fusion.1
  673.1 10.2 %all-reduce.1 = (f32[2]{0:T(128)S(1)}, f32[2]{0:T(128)S(1)}, f32[2]{0:T(128)S(1)}) all-reduce(f32[2]{0:T(128)S(1)} %pad_maximum_fusion.3, f32[2]{0:T(128)S(1)} %get-tuple-element.32, f32[2]{0:T(128)S(1)} %get-tuple-element.31), channel_id=1, replica_groups=mesh['tok_0'=4,'tok_1'=2,'tok_2'=2,'col_0'=2,'col_1'=4] {'tok_0'}, use_global_device_ids=true, to_apply=%region_18.19 | all-reduce | flops 6 | bytes 48 | tf_op jit(solution)/shard_map/psum | solution.py:33
  683.3 4.9 all-reduce.4
  688.2 2.4 all-reduce.3
  690.7 6.4 all-reduce.2
  697.1 9.0 %all-reduce = (f32[2]{0:T(128)S(1)}, f32[2]{0:T(128)S(1)}, f32[2]{0:T(128)S(1)}) all-reduce(f32[2]{0:T(128)S(1)} %get-tuple-element.14, f32[2]{0:T(128)S(1)} %get-tuple-element.15, f32[2]{0:T(128)S(1)} %get-tuple-element.16), channel_id=1, replica_groups=mesh['tok_0'=4,'tok_1'=2,'tok_2'=2,'col_0'=2,'col_1'=4] {'col_1'}, use_global_device_ids=true, to_apply=%region_22.23 | all-reduce | flops 6 | bytes 48 | tf_op jit(solution)/shard_map/psum | solution.py:33
  (20 shorter events, 2.0 us)
Async XLA Ops:
  8.5 11.6 %all-to-all-start.1 = ((s32[16,1,256]{2,1,0:T(1,128)}), s32[16,1,256]{2,1,0:T(1,128)S(1)}, u32[]{:S(2)}, u32[]{:S(2)}) async-start(s32[16,1,256]{2,1,0:T(1,128)} %broadcast_in_dim.2), calls=%async_computation.1 | async-start | bytes 32768 | tf_op jit(solution)/shard_map/all_to_all | solution.py:18
  25.6 7.8 %copy-start = (s32[2,1536]{1,0:T(2,128)S(1)}, s32[2,1536]{1,0:T(2,128)}, u32[]{:S(2)}) copy-start(s32[2,1536]{1,0:T(2,128)} %param.9) | copy-start | bytes 36868
  25.6 146.9 %all-to-all-start.4 = ((bf16[8,1536,512]{1,2,0:T(8,128)(2,1)}), bf16[8,1536,512]{1,2,0:T(8,128)(2,1)}, u32[]{:S(2)}, u32[]{:S(2)}) async-start(bf16[8,1536,512]{1,2,0:T(8,128)(2,1)} %stack.39), calls=%async_computation.5 | async-start | bytes 25165824 | tf_op jit(solution)/shard_map/all_to_all | solution.py:66
  33.4 482.6 %reduce-scatter.5.cloned.1.call-start = ((), (), s32[]{:S(2)}) async-start(), calls=%async_computation.10 | async-start | bytes 8912896 | tf_op jit(solution)/shard_map/reduce_scatter | solution.py:81
  227.2 385.4 %reduce-scatter.3.cloned.1.call-start = ((), (), s32[]{:S(2)}) async-start(), calls=%async_computation.9 | async-start | bytes 8912896 | tf_op jit(solution)/shard_map/reduce_scatter | solution.py:81
  233.5 225.2 %copy-start.3 = (bf16[2,1536,512]{2,1,0:T(8,128)(2,1)S(1)}, bf16[2,1536,512]{2,1,0:T(8,128)(2,1)}, u32[]{:S(2)}) copy-start(bf16[2,1536,512]{2,1,0:T(8,128)(2,1)} %param.8) | copy-start | bytes 9437188
  515.4 0.7 copy-start.1
  520.4 96.6 %all-to-all-start.5 = ((f32[8,32,512]{2,1,0:T(8,128)}), f32[8,32,512]{2,1,0:T(8,128)S(1)}, u32[]{:S(2)}, u32[]{:S(2)}) async-start(f32[8,32,512]{2,1,0:T(8,128)} %bitcast.20), calls=%async_computation.7 | async-start | bytes 1048576 | tf_op jit(solution)/shard_map/all_to_all | solution.py:91
  524.1 130.2 %copy-start.2 = (s32[2]{0:T(128)S(1)}, s32[2]{0:T(128)}, u32[]{:S(2)}) copy-start(s32[2]{0:T(128)} %param.13) | copy-start | bytes 28
  616.9 17.6 %all-to-all-start.2 = ((f32[8,32,512]{2,1,0:T(8,128)}), f32[8,32,512]{2,1,0:T(8,128)S(1)}, u32[]{:S(2)}, u32[]{:S(2)}) async-start(f32[8,32,512]{2,1,0:T(8,128)} %bitcast.11), calls=%async_computation.3 | async-start | bytes 1048576 | tf_op jit(solution)/shard_map/all_to_all | solution.py:91
  634.6 16.2 %all-to-all-start.6 = ((f32[8,32,512]{2,1,0:T(8,128)}), f32[8,32,512]{2,1,0:T(8,128)S(1)}, u32[]{:S(2)}, u32[]{:S(2)}) async-start(f32[8,32,512]{2,1,0:T(8,128)} %copy.30), calls=%async_computation.8 | async-start | bytes 1048576 | tf_op jit(solution)/shard_map/all_to_all | solution.py:93
  650.8 14.5 %all-to-all-start.3 = ((f32[8,32,512]{2,1,0:T(8,128)}), f32[8,32,512]{2,1,0:T(8,128)S(1)}, u32[]{:S(2)}, u32[]{:S(2)}) async-start(f32[8,32,512]{2,1,0:T(8,128)} %copy.25), calls=%async_computation.4 | async-start | bytes 1048576 | tf_op jit(solution)/shard_map/all_to_all | solution.py:93
Sparse Core Ops, SparseCore 0:
  227.3 167.9 reduce-scatter.4
  515.5 97.0 reduce-scatter.2
